TPU v7x, 32 devices: a whole 2x2x4 slice. The times are simulated.
32 devices in a mesh: pool: 4 (over x, core), rp: 8 (over z, y).
Axes of the slice: x: 2, y: 2, z: 4, core: 2. Of those that a mesh axis runs over, the one named last changes fastest.
Arguments:
- wannier_coupling: bfloat16 [2, 512, 5184], P(None, ('pool', 'rp')), may hold values from -0.25 to 0.25
- lattice_vectors: int32 [3, 512], P(None, ('pool', 'rp')), may hold values from -12 to 12
- degeneracy: int32 [1, 512], P(None, ('pool', 'rp')), may hold values from 1 to 4
- fine_points: int32 [3, 32], P(None, 'pool'), may hold values from 0 to 47
- mode_vectors: float32 [32, 2, 9, 9], P('pool'), may hold values from -2 to 2
- bands_shifted: float32 [32, 2, 24, 24], P(('pool', 'rp')), may hold values from -1.25 to 1.25
- bands_anchor: float32 [2, 24, 24], replicated, may hold values from -1.25 to 1.25
Outputs:
- coupling: float32 [32, 2, 9, 576], P(('pool', 'rp'))
All inputs are finite; a program needn't handle non-finite values.
Results may differ from a plain program's by a relative error of at most 0.0021.
Values may be sent and summed in bfloat16 or wider, within the bound.
A program may use at most 64 MiB of HBM per device.

v0:
```python
import math
import jax
import jax.numpy as jnp
from jax import lax
from jax.sharding import PartitionSpec as P

NQG = 48
full_turn = 2.0 * math.pi
highest = lax.Precision.HIGHEST


def phase_pair(fine_points, lattice_vectors, degeneracy):
    winding = fine_points[0][:, None] * lattice_vectors[0][None, :]
    winding = winding + fine_points[1][:, None] * lattice_vectors[1][None, :]
    winding = winding + fine_points[2][:, None] * lattice_vectors[2][None, :]
    winding = jnp.mod(winding, NQG)
    angles = winding.astype(jnp.float32) * (full_turn / NQG)
    weights = 1.0 / degeneracy[0].astype(jnp.float32)
    phase_real = (jnp.cos(angles) * weights[None, :]).astype(jnp.bfloat16)
    phase_imag = (jnp.sin(angles) * weights[None, :]).astype(jnp.bfloat16)
    return (phase_real, phase_imag)


def contract_modes(source, matrix):
    return jnp.einsum("qap,qav->qvp", source, matrix, precision=highest)


def rotate_modes(real_part, imag_part, vectors):
    vector_real = vectors[:, 0]
    vector_imag = vectors[:, 1]
    out_real = contract_modes(real_part, vector_real) - contract_modes(imag_part, vector_imag)
    out_imag = contract_modes(real_part, vector_imag) + contract_modes(imag_part, vector_real)
    return (out_real, out_imag)


def rotate_bands(real_part, imag_part, shifted, anchor):
    points = real_part.shape[0]
    mode_count = real_part.shape[1]
    band_count = anchor.shape[1]
    grid_real = real_part.reshape(points, mode_count, band_count, band_count)
    grid_imag = imag_part.reshape(points, mode_count, band_count, band_count)

    def right_product(source, matrix):
        return jnp.einsum("qvmn,nl->qvml", source, matrix, precision=highest)

    def left_product(matrix, source):
        return jnp.einsum("qma,qvml->qval", matrix, source, precision=highest)

    right_real = right_product(grid_real, anchor[0]) - right_product(grid_imag, anchor[1])
    right_imag = right_product(grid_real, anchor[1]) + right_product(grid_imag, anchor[0])
    shift_real = shifted[:, 0]
    shift_imag = shifted[:, 1]
    final_real = left_product(shift_real, right_real) + left_product(shift_imag, right_imag)
    final_imag = left_product(shift_real, right_imag) - left_product(shift_imag, right_real)
    final_real = final_real.reshape(points, mode_count, band_count * band_count)
    final_imag = final_imag.reshape(points, mode_count, band_count * band_count)
    return jnp.stack([final_real, final_imag], axis=1)


def fold_groups(coupling_block, vectors_block, weights_block, fine_points):
    coupling_rows = lax.all_gather(coupling_block, "pool", axis=1, tiled=True)
    vectors_here = lax.all_gather(vectors_block, "pool", axis=1, tiled=True)
    degeneracy_here = lax.all_gather(weights_block, "pool", axis=1, tiled=True)
    phase_real, phase_imag = phase_pair(fine_points, vectors_here, degeneracy_here)
    real_sum = jnp.dot(phase_real, coupling_rows[0], preferred_element_type=jnp.float32) - jnp.dot(
        phase_imag, coupling_rows[1], preferred_element_type=jnp.float32
    )
    imag_sum = jnp.dot(phase_real, coupling_rows[1], preferred_element_type=jnp.float32) + jnp.dot(
        phase_imag, coupling_rows[0], preferred_element_type=jnp.float32
    )
    return (real_sum, imag_sum)


def finish_owner(part_real, part_imag, mode_vectors, bands_shifted, bands_anchor):
    mode_real, mode_imag = rotate_modes(part_real, part_imag, mode_vectors)
    return rotate_bands(
        lax.all_to_all(mode_real, "rp", split_axis=0, concat_axis=2, tiled=True),
        lax.all_to_all(mode_imag, "rp", split_axis=0, concat_axis=2, tiled=True),
        bands_shifted,
        bands_anchor,
    )


def per_device(
    wannier_coupling,
    lattice_vectors,
    degeneracy,
    fine_points,
    mode_vectors,
    bands_shifted,
    bands_anchor,
):
    points = fine_points.shape[1]
    mode_count = mode_vectors.shape[2]
    pair_count = bands_anchor.shape[1] * bands_anchor.shape[2]
    rows_here = wannier_coupling.shape[1]
    shaped = wannier_coupling.reshape(2, rows_here, mode_count, pair_count)
    moved = lax.all_to_all(shaped, "rp", split_axis=3, concat_axis=1, tiled=True)
    group_rows = moved.shape[1]
    moved = moved.reshape(2, group_rows, -1)
    vectors_group, weights_group = (
        lax.all_gather(lattice_vectors, "rp", axis=1, tiled=True),
        lax.all_gather(degeneracy, "rp", axis=1, tiled=True),
    )
    sum_real, sum_imag = fold_groups(moved, vectors_group, weights_group, fine_points)
    part_real = sum_real.reshape(points, mode_count, -1)
    part_imag = sum_imag.reshape(points, mode_count, -1)
    return finish_owner(part_real, part_imag, mode_vectors, bands_shifted, bands_anchor)


def solution(mesh):
    return jax.shard_map(
        per_device,
        mesh=mesh,
        in_specs=(
            P(None, ("pool", "rp"), None),
            P(None, ("pool", "rp")),
            P(None, ("pool", "rp")),
            P(None, "pool"),
            P("pool", None, None, None),
            P(("pool", "rp"), None, None, None),
            P(),
        ),
        out_specs=P(("pool", "rp"), None, None, None),
        check_vma=False,
    )
```

profile of v0, /device:TPU:0, one launch (start us, length us, event | category | flops | bytes accessed | tf_op | source)
XLA Modules:
  0.0 130.1 jit_solution(11146342148523568554)
XLA Ops:
  6.5 1.3 %reshape.64 = bf16[2,16,9,576]{3,2,1,0:T(8,128)(2,1)S(1)} reshape(bf16[2,16,5184]{2,1,0:T(8,128)(2,1)} %param.7) | data formatting | bytes 663552 | tf_op jit(solution)/shard_map/reshape | solution.py:97
  7.9 8.5 %copy.44 = bf16[2,16,9,576]{1,0,2,3:T(2,128)(2,1)S(1)} copy(bf16[2,16,9,576]{3,2,1,0:T(8,128)(2,1)S(1)} %reshape.64) | data formatting | bytes 663552 | tf_op jit(solution)/shard_map/reshape | solution.py:97
  16.4 2.7 %reshape.83 = bf16[8,2,10368]{2,1,0:T(2,128)(2,1)S(1)} reshape(bf16[576,9,2,16]{3,2,1,0:T(2,128)(2,1)S(1)} %bitcast.111) | data formatting | bytes 663552
  19.1 18.1 %all_to_all.45 = bf16[8,2,10368]{2,1,0:T(2,128)(2,1)S(1)} all-to-all(bf16[8,2,10368]{2,1,0:T(2,128)(2,1)S(1)} %reshape.83), channel_id=1, replica_groups=mesh['pool'=4,'rp'=8] {'rp'}, dimensions={0} | all-to-all | bytes 663552 | tf_op jit(solution)/shard_map/all_to_all | solution.py:98
  37.2 1.9 %reshape.84 = bf16[576,9,2,16]{3,2,1,0:T(2,128)(2,1)S(1)} reshape(bf16[8,2,10368]{2,1,0:T(2,128)(2,1)S(1)} %all_to_all.45) | data formatting | bytes 663552
  39.1 4.1 %copy.63 = bf16[2,16,9,8,72]{4,2,1,3,0:T(8,128)(2,1)} copy(bf16[2,16,9,8,72]{1,0,2,4,3:T(2,128)(2,1)S(1)} %bitcast.112) | data formatting | bytes 663552 | tf_op jit(solution)/shard_map/all_to_all | solution.py:98
  43.2 2.6 %reshape.65 = bf16[2,128,648]{2,1,0:T(8,128)(2,1)} reshape(bf16[2,8,16,9,72]{4,3,2,1,0:T(8,128)(2,1)} %bitcast.113) | data formatting | bytes 663552 | tf_op jit(solution)/shard_map/reshape | solution.py:100
  45.9 26.1 %all-gather = s32[8,16,3]{1,2,0:T(4,128)S(1)} all-gather(s32[1,16,3]{1,2,0:T(4,128)S(1)} %bitcast.117), channel_id=1, replica_groups=mesh['pool'=4,'rp'=8] {'rp'}, dimensions={0}, use_global_device_ids=true | all-gather | bytes 1728 | tf_op jit(solution)/shard_map/all_gather | solution.py:102
  72.1 0.1 copy.64
  72.3 0.1 copy.65
  72.4 0.6 dynamic-slice
  73.7 0.1 bitcast_dynamic-update-slice_fusion
  73.8 7.7 %all-reduce = s32[128]{0:T(128)S(1)} all-reduce(s32[128]{0:T(128)S(1)} %bitcast_dynamic-update-slice_fusion), channel_id=1, replica_groups=mesh['pool'=4,'rp'=8] {'rp'}, use_global_device_ids=true, to_apply=%add | all-reduce | flops 128 | bytes 1024
  81.5 5.0 %all_gather.18 = s32[1,512]{1,0:T(1,128)S(1)} all-gather(s32[1,128]{1,0:T(1,128)S(1)} %bitcast.134), channel_id=1, replica_groups=mesh['pool'=4,'rp'=8] {'pool'}, dimensions={1}, use_global_device_ids=true | all-gather | bytes 2560 | tf_op jit(solution)/shard_map/all_gather | solution.py:63
  86.5 5.2 %all_gather.16 = s32[3,512]{1,0:T(4,128)S(1)} all-gather(s32[3,128]{1,0:T(4,128)S(1)} %bitcast.116), channel_id=1, replica_groups=mesh['pool'=4,'rp'=8] {'pool'}, dimensions={1}, use_global_device_ids=true | all-gather | bytes 7680 | tf_op jit(solution)/shard_map/all_gather | solution.py:62
  91.7 1.6 %fusion.4 = f32[8,648]{1,0:T(8,128)S(1)} fusion(bf16[2,512,648]{2,1,0:T(8,128)(2,1)} %all-gather.3.cloned.1.call-done, f32[512]{0:T(512)S(1)} %bitcast.118, s32[512]{0:T(512)S(1)} %bitcast.126, s32[8]{0:T(128)S(1)} %get-tuple-element.11, s32[512]{0:T(512)S(1)} %bitcast.130, s32[8]{0:T(128)S(1)} %get-tuple-element.12, s32[512]{0:T(512)S(1)} %bitcast.122, ...), kind=kOutput, calls=%fused_computation.14 | convolution fusion | flops 5369856 | bytes 815456 | tf_op jit(solution)/shard_map/dot_general | solution.py:65
  93.3 1.5 %convolution_subtract_fusion.3 = f32[8,648]{1,0:T(8,128)S(1)} fusion(f32[8,648]{1,0:T(8,128)S(1)} %fusion.4, bf16[2,512,648]{2,1,0:T(8,128)(2,1)} %all-gather.3.cloned.1.call-done, f32[512]{0:T(512)S(1)} %bitcast.119, s32[512]{0:T(512)S(1)} %bitcast.127, s32[8]{0:T(128)S(1)} %get-tuple-element.11, s32[512]{0:T(512)S(1)} %bitcast.131, ...), kind=kOutput, calls=%fused_computation.11 | convolution fusion | flops 5375040 | bytes 836192 | tf_op jit(solution)/shard_map/dot_general | solution.py:65
  94.8 0.1 reshape.66
  94.9 0.3 fusion.5
  95.2 0.3 convolution_add_fusion.3
  95.6 0.1 reshape.67
  95.7 0.2 fusion.10
  95.9 0.2 fusion.6
  96.1 0.2 fusion.3
  96.3 0.7 reshape.85
  97.0 5.4 %all-to-all-start.1 = ((f32[8,1,648]{2,1,0:T(1,128)}), f32[8,1,648]{2,1,0:T(1,128)S(1)}, u32[]{:S(2)}, u32[]{:S(2)}) async-start(f32[8,1,648]{2,1,0:T(1,128)} %reshape.85), calls=%async_computation.1 | async-start | bytes 49152 | tf_op jit(solution)/shard_map/all_to_all | solution.py:77
  102.5 0.2 fusion.2
  102.7 0.7 reshape.87
  103.4 5.7 %all-to-all-done.1 = f32[8,1,648]{2,1,0:T(1,128)S(1)} async-done(((f32[8,1,648]{2,1,0:T(1,128)}), f32[8,1,648]{2,1,0:T(1,128)S(1)}, u32[]{:S(2)}, u32[]{:S(2)}) %all-to-all-start.1) | async-done | bytes 20768 | tf_op jit(solution)/shard_map/all_to_all | solution.py:77
  109.1 3.3 %all-to-all-start.2 = ((f32[8,1,648]{2,1,0:T(1,128)}), f32[8,1,648]{2,1,0:T(1,128)S(1)}, u32[]{:S(2)}, u32[]{:S(2)}) async-start(f32[8,1,648]{2,1,0:T(1,128)} %reshape.87), calls=%async_computation.2 | async-start | bytes 49152 | tf_op jit(solution)/shard_map/all_to_all | solution.py:78
  112.4 0.5 broadcast.4
  112.9 0.7 reduce
  113.8 0.1 reshape.68
  113.9 0.3 fusion.23
  114.2 0.3 fusion.27
  114.5 4.5 %all-to-all-done.2 = f32[8,1,648]{2,1,0:T(1,128)S(1)} async-done(((f32[8,1,648]{2,1,0:T(1,128)}), f32[8,1,648]{2,1,0:T(1,128)S(1)}, u32[]{:S(2)}, u32[]{:S(2)}) %all-to-all-start.2) | async-done | bytes 20768 | tf_op jit(solution)/shard_map/all_to_all | solution.py:78
  119.0 0.7 reduce.1
  119.8 0.1 reshape.69
  119.9 0.3 convolution_add_fusion.1
  120.2 0.3 convolution_subtract_fusion.1
  120.6 0.4 fusion.19
  120.9 0.4 fusion.21
  121.3 0.4 fusion
  121.7 0.1 copy.56
  121.8 0.1 stack_reshape.7
  122.0 0.4 fusion.1
  122.4 0.1 stack_reshape.6
  122.6 0.6 copy.57
  (32 shorter events, 0.6 us)
Async XLA Ops:
  6.5 85.2 %all-gather.3.cloned.1.call-start = ((), (), s32[]{:S(2)}) async-start(), calls=%async_computation.3 | async-start | bytes 1966080 | tf_op jit(solution)/shard_map/all_gather | solution.py:61
  43.2 2.7 %copy-start.3 = (s32[3,16]{1,0:T(4,128)S(1)}, s32[3,16]{1,0:T(4,128)}, u32[]{:S(2)}) copy-start(s32[3,16]{1,0:T(4,128)} %param.8) | copy-start | bytes 580
  43.2 28.9 %copy-start.2 = (f32[8,2,9,9]{3,1,2,0:T(2,128)S(1)}, f32[8,2,9,9]{3,1,2,0:T(2,128)}, u32[]{:S(2)}) copy-start(f32[8,2,9,9]{3,1,2,0:T(2,128)} %param.11) | copy-start | bytes 15556
  43.2 29.2 %copy-start.7 = (u32[32]{0:T(128)S(1)}, u32[32]{0:T(128)}, u32[]{:S(2)}) copy-start(u32[32]{0:T(128)} %constant.22) | copy-start | bytes 388
  43.2 30.5 %copy-start.6 = (s32[1,16]{1,0:T(1,128)S(1)}, s32[1,16]{1,0:T(1,128)}, u32[]{:S(2)}) copy-start(s32[1,16]{1,0:T(1,128)} %param.9) | copy-start | bytes 196
  43.2 48.5 %copy-start.4 = (s32[3,8]{1,0:T(4,128)S(1)}, s32[3,8]{1,0:T(4,128)}, u32[]{:S(2)}) copy-start(s32[3,8]{1,0:T(4,128)} %param.10) | copy-start | bytes 292
  91.7 3.2 %copy-start.5 = (bf16[2,512,648]{2,1,0:T(8,128)(2,1)S(1)}, bf16[2,512,648]{2,1,0:T(8,128)(2,1)}, u32[]{:S(2)}) copy-start(bf16[2,512,648]{2,1,0:T(8,128)(2,1)} %all-gather.3.cloned.1.call-done) | copy-start | bytes 3981316
  94.9 19.0 %copy-start = (f32[2,24,24]{2,1,0:T(8,128)S(1)}, f32[2,24,24]{2,1,0:T(8,128)}, u32[]{:S(2)}) copy-start(f32[2,24,24]{2,1,0:T(8,128)} %param.13) | copy-start | bytes 13828
  95.7 24.9 %copy-start.1 = (f32[1,2,24,24]{3,2,1,0:T(8,128)S(1)}, f32[1,2,24,24]{3,2,1,0:T(8,128)}, u32[]{:S(2)}) copy-start(f32[1,2,24,24]{3,2,1,0:T(8,128)} %param.12) | copy-start | bytes 13828
  97.0 12.1 %all-to-all-start.1 = ((f32[8,1,648]{2,1,0:T(1,128)}), f32[8,1,648]{2,1,0:T(1,128)S(1)}, u32[]{:S(2)}, u32[]{:S(2)}) async-start(f32[8,1,648]{2,1,0:T(1,128)} %reshape.85), calls=%async_computation.1 | async-start | bytes 49152 | tf_op jit(solution)/shard_map/all_to_all | solution.py:77
  109.1 9.9 %all-to-all-start.2 = ((f32[8,1,648]{2,1,0:T(1,128)}), f32[8,1,648]{2,1,0:T(1,128)S(1)}, u32[]{:S(2)}, u32[]{:S(2)}) async-start(f32[8,1,648]{2,1,0:T(1,128)} %reshape.87), calls=%async_computation.2 | async-start | bytes 49152 | tf_op jit(solution)/shard_map/all_to_all | solution.py:78
Sparse Core Ops, SparseCore 0:
  46.0 18.0 all-gather.2
where the time goes:
time: 131 us; the launch traced here: 130 us
  blocking collectives  62.1 us (47%)
  local copies, waits for them, and re-layouts  25.9 us (20%)
  between operations  14.4 us (11%)
  waiting for transfers between devices  10.2 us (8%)
  starting transfers between devices  8.75 us (7%)
  matrix products  7.26 us (6%)
  other arithmetic  1.46 us (1%)
    all_gather x1, blocking collectives, per_device(): lax.all_gather(lattice_vectors, 'rp', axis=1, tiled=True)  26.1 us
    all_to_all x1, blocking collectives, per_device(): lax.all_to_all(shaped, 'rp', split_axis=3, concat_axis=1, tiled=True)  18.1 us
    reshape x2, local copies, waits for them, and re-layouts, per_device(): shaped = wannier_coupling.reshape(2, rows_here, mode_count, pair_count)  9.81 us
    unnamed x1, blocking collectives  7.67 us
    unnamed x28, local copies, waits for them, and re-layouts  7.31 us
    all_to_all x1, waiting for transfers between devices, finish_owner(): lax.all_to_all(mode_real, 'rp', split_axis=0, concat_axis=2, tiled=True)  5.72 us
    all_to_all x1, starting transfers between devices, finish_owner(): lax.all_to_all(mode_real, 'rp', split_axis=0, concat_axis=2, tiled=True)  5.44 us
    all_gather x1, blocking collectives, fold_groups(): vectors_here = lax.all_gather(vectors_block, 'pool', axis=1, tiled=True)  5.18 us
  transfers between devices with their start and end apart: 3, of which 2 were waited for; matrix products, arithmetic and copies ran while one was open for 3% of the time, Pallas kernels for 0%

commit v1 on v0

--- a/solution.py
+++ b/solution.py
@@ -59,8 +59,13 @@
 
 def fold_groups(coupling_block, vectors_block, weights_block, fine_points):
     coupling_rows = lax.all_gather(coupling_block, "pool", axis=1, tiled=True)
-    vectors_here = lax.all_gather(vectors_block, "pool", axis=1, tiled=True)
-    degeneracy_here = lax.all_gather(weights_block, "pool", axis=1, tiled=True)
+    vectors_here, degeneracy_here = jnp.split(
+        lax.all_gather(
+            jnp.concatenate([vectors_block, weights_block], axis=0), "pool", axis=1, tiled=True
+        ),
+        [vectors_block.shape[0]],
+        axis=0,
+    )
     phase_real, phase_imag = phase_pair(fine_points, vectors_here, degeneracy_here)
     real_sum = jnp.dot(phase_real, coupling_rows[0], preferred_element_type=jnp.float32) - jnp.dot(
         phase_imag, coupling_rows[1], preferred_element_type=jnp.float32

time: 131 us -> 126 us (0.962)
  blocking collectives: 62.1 us -> 57.1 us
    all_gather x2 -> x1, blocking collectives: 10.2 us -> 5.19 us  [fold_groups(): lax.all_gather(jnp.concatenate([vectors_block, weights_block], axis=0), '...]
where the time goes in v1:
time: 126 us; the launch traced here: 125 us
  blocking collectives  57.1 us (45%)
  local copies, waits for them, and re-layouts  25.9 us (21%)
  between operations  14.4 us (11%)
  waiting for transfers between devices  10.2 us (8%)
  starting transfers between devices  8.74 us (7%)
  matrix products  7.26 us (6%)
  other arithmetic  1.47 us (1%)
    all_gather x1, blocking collectives, per_device(): lax.all_gather(lattice_vectors, 'rp', axis=1, tiled=True)  26.1 us
    all_to_all x1, blocking collectives, per_device(): lax.all_to_all(shaped, 'rp', split_axis=3, concat_axis=1, tiled=True)  18.1 us
    reshape x2, local copies, waits for them, and re-layouts, per_device(): shaped = wannier_coupling.reshape(2, rows_here, mode_count, pair_count)  9.81 us
    unnamed x1, blocking collectives  7.67 us
    unnamed x28, local copies, waits for them, and re-layouts  7.31 us
    all_to_all x1, waiting for transfers between devices, finish_owner(): lax.all_to_all(mode_real, 'rp', split_axis=0, concat_axis=2, tiled=True)  5.72 us
    all_to_all x1, starting transfers between devices, finish_owner(): lax.all_to_all(mode_real, 'rp', split_axis=0, concat_axis=2, tiled=True)  5.43 us
    all_gather x1, blocking collectives, fold_groups(): lax.all_gather(jnp.concatenate([vectors_block, weights_block], axis=0), '...  5.19 us
  transfers between devices with their start and end apart: 3, of which 2 were waited for; matrix products, arithmetic and copies ran while one was open for 3% of the time, Pallas kernels for 0%

profile of v1, /device:TPU:0, one launch (start us, length us, event | category | flops | bytes accessed | tf_op | source)
XLA Modules:
  0.0 125.1 jit_solution(2644385963509724571)
XLA Ops:
  6.5 1.3 %reshape.64 = bf16[2,16,9,576]{3,2,1,0:T(8,128)(2,1)S(1)} reshape(bf16[2,16,5184]{2,1,0:T(8,128)(2,1)} %param.7) | data formatting | bytes 663552 | tf_op jit(solution)/shard_map/reshape | solution.py:102
  7.9 8.5 %copy.45 = bf16[2,16,9,576]{1,0,2,3:T(2,128)(2,1)S(1)} copy(bf16[2,16,9,576]{3,2,1,0:T(8,128)(2,1)S(1)} %reshape.64) | data formatting | bytes 663552 | tf_op jit(solution)/shard_map/reshape | solution.py:102
  16.4 2.7 %reshape.83 = bf16[8,2,10368]{2,1,0:T(2,128)(2,1)S(1)} reshape(bf16[576,9,2,16]{3,2,1,0:T(2,128)(2,1)S(1)} %bitcast.111) | data formatting | bytes 663552
  19.1 18.1 %all_to_all.45 = bf16[8,2,10368]{2,1,0:T(2,128)(2,1)S(1)} all-to-all(bf16[8,2,10368]{2,1,0:T(2,128)(2,1)S(1)} %reshape.83), channel_id=1, replica_groups=mesh['pool'=4,'rp'=8] {'rp'}, dimensions={0} | all-to-all | bytes 663552 | tf_op jit(solution)/shard_map/all_to_all | solution.py:103
  37.2 1.9 %reshape.84 = bf16[576,9,2,16]{3,2,1,0:T(2,128)(2,1)S(1)} reshape(bf16[8,2,10368]{2,1,0:T(2,128)(2,1)S(1)} %all_to_all.45) | data formatting | bytes 663552
  39.1 4.1 %copy.64 = bf16[2,16,9,8,72]{4,2,1,3,0:T(8,128)(2,1)} copy(bf16[2,16,9,8,72]{1,0,2,4,3:T(2,128)(2,1)S(1)} %bitcast.112) | data formatting | bytes 663552 | tf_op jit(solution)/shard_map/all_to_all | solution.py:103
  43.2 2.6 %reshape.65 = bf16[2,128,648]{2,1,0:T(8,128)(2,1)} reshape(bf16[2,8,16,9,72]{4,3,2,1,0:T(8,128)(2,1)} %bitcast.113) | data formatting | bytes 663552 | tf_op jit(solution)/shard_map/reshape | solution.py:105
  45.9 26.1 %all-gather = s32[8,16,3]{1,2,0:T(4,128)S(1)} all-gather(s32[1,16,3]{1,2,0:T(4,128)S(1)} %bitcast.117), channel_id=1, replica_groups=mesh['pool'=4,'rp'=8] {'rp'}, dimensions={0}, use_global_device_ids=true | all-gather | bytes 1728 | tf_op jit(solution)/shard_map/all_gather | solution.py:107
  72.1 0.1 copy.65
  72.3 0.1 copy.66
  72.4 0.6 dynamic-slice
  73.7 0.1 bitcast_dynamic-update-slice_fusion
  73.8 7.7 %all-reduce = s32[128]{0:T(128)S(1)} all-reduce(s32[128]{0:T(128)S(1)} %bitcast_dynamic-update-slice_fusion), channel_id=1, replica_groups=mesh['pool'=4,'rp'=8] {'rp'}, use_global_device_ids=true, to_apply=%add | all-reduce | flops 128 | bytes 1024
  81.5 5.2 %all_gather.14 = s32[4,512]{1,0:T(4,128)S(1)} all-gather(s32[4,128]{1,0:T(4,128)S(1)} %pad_add_fusion), channel_id=1, replica_groups=mesh['pool'=4,'rp'=8] {'pool'}, dimensions={1}, use_global_device_ids=true | all-gather | bytes 10240 | tf_op jit(solution)/shard_map/all_gather | solution.py:63
  86.7 1.6 %fusion.4 = f32[8,648]{1,0:T(8,128)S(1)} fusion(bf16[2,512,648]{2,1,0:T(8,128)(2,1)} %all-gather.3.cloned.1.call-done, f32[512]{0:T(512)S(1)} %bitcast.118, s32[512]{0:T(512)S(1)} %bitcast.126, s32[8]{0:T(128)S(1)} %get-tuple-element.11, s32[512]{0:T(512)S(1)} %bitcast.130, s32[8]{0:T(128)S(1)} %get-tuple-element.12, s32[512]{0:T(512)S(1)} %bitcast.122, ...), kind=kOutput, calls=%fused_computation.14 | convolution fusion | flops 5369856 | bytes 815456 | tf_op jit(solution)/shard_map/dot_general | solution.py:70
  88.3 1.5 %convolution_subtract_fusion.3 = f32[8,648]{1,0:T(8,128)S(1)} fusion(f32[8,648]{1,0:T(8,128)S(1)} %fusion.4, bf16[2,512,648]{2,1,0:T(8,128)(2,1)} %all-gather.3.cloned.1.call-done, f32[512]{0:T(512)S(1)} %bitcast.119, s32[512]{0:T(512)S(1)} %bitcast.127, s32[8]{0:T(128)S(1)} %get-tuple-element.11, s32[512]{0:T(512)S(1)} %bitcast.131, ...), kind=kOutput, calls=%fused_computation.11 | convolution fusion | flops 5375040 | bytes 836192 | tf_op jit(solution)/shard_map/dot_general | solution.py:70
  89.8 0.1 reshape.66
  89.9 0.3 fusion.5
  90.2 0.3 convolution_add_fusion.3
  90.6 0.1 reshape.67
  90.7 0.2 fusion.10
  90.9 0.2 fusion.6
  91.1 0.2 fusion.3
  91.3 0.7 reshape.85
  92.0 5.4 %all-to-all-start.1 = ((f32[8,1,648]{2,1,0:T(1,128)}), f32[8,1,648]{2,1,0:T(1,128)S(1)}, u32[]{:S(2)}, u32[]{:S(2)}) async-start(f32[8,1,648]{2,1,0:T(1,128)} %reshape.85), calls=%async_computation.1 | async-start | bytes 49152 | tf_op jit(solution)/shard_map/all_to_all | solution.py:82
  97.5 0.2 fusion.2
  97.7 0.7 reshape.87
  98.4 5.7 %all-to-all-done.1 = f32[8,1,648]{2,1,0:T(1,128)S(1)} async-done(((f32[8,1,648]{2,1,0:T(1,128)}), f32[8,1,648]{2,1,0:T(1,128)S(1)}, u32[]{:S(2)}, u32[]{:S(2)}) %all-to-all-start.1) | async-done | bytes 20768 | tf_op jit(solution)/shard_map/all_to_all | solution.py:82
  104.1 3.3 %all-to-all-start.2 = ((f32[8,1,648]{2,1,0:T(1,128)}), f32[8,1,648]{2,1,0:T(1,128)S(1)}, u32[]{:S(2)}, u32[]{:S(2)}) async-start(f32[8,1,648]{2,1,0:T(1,128)} %reshape.87), calls=%async_computation.2 | async-start | bytes 49152 | tf_op jit(solution)/shard_map/all_to_all | solution.py:83
  107.4 0.5 broadcast.4
  107.9 0.7 reduce
  108.7 0.1 reshape.68
  108.8 0.3 fusion.23
  109.2 0.3 fusion.27
  109.5 4.5 %all-to-all-done.2 = f32[8,1,648]{2,1,0:T(1,128)S(1)} async-done(((f32[8,1,648]{2,1,0:T(1,128)}), f32[8,1,648]{2,1,0:T(1,128)S(1)}, u32[]{:S(2)}, u32[]{:S(2)}) %all-to-all-start.2) | async-done | bytes 20768 | tf_op jit(solution)/shard_map/all_to_all | solution.py:83
  114.0 0.7 reduce.1
  114.8 0.1 reshape.69
  114.9 0.3 convolution_add_fusion.1
  115.2 0.3 convolution_subtract_fusion.1
  115.5 0.4 fusion.19
  115.9 0.4 fusion.21
  116.3 0.4 fusion
  116.7 0.1 copy.57
  116.8 0.1 stack_reshape.7
  116.9 0.4 fusion.1
  117.3 0.1 copy.54
  117.4 0.1 stack_reshape.6
  117.6 0.6 copy.58
  (32 shorter events, 0.5 us)
Async XLA Ops:
  6.5 80.2 %all-gather.3.cloned.1.call-start = ((), (), s32[]{:S(2)}) async-start(), calls=%async_computation.3 | async-start | bytes 1966080 | tf_op jit(solution)/shard_map/all_gather | solution.py:61
  43.2 2.7 %copy-start.3 = (s32[3,16]{1,0:T(4,128)S(1)}, s32[3,16]{1,0:T(4,128)}, u32[]{:S(2)}) copy-start(s32[3,16]{1,0:T(4,128)} %param.8) | copy-start | bytes 580
  43.2 28.9 %copy-start.2 = (f32[8,2,9,9]{3,1,2,0:T(2,128)S(1)}, f32[8,2,9,9]{3,1,2,0:T(2,128)}, u32[]{:S(2)}) copy-start(f32[8,2,9,9]{3,1,2,0:T(2,128)} %param.11) | copy-start | bytes 15556
  43.2 29.2 %copy-start.7 = (u32[32]{0:T(128)S(1)}, u32[32]{0:T(128)}, u32[]{:S(2)}) copy-start(u32[32]{0:T(128)} %constant.22) | copy-start | bytes 388
  43.2 30.5 %copy-start.6 = (s32[1,16]{1,0:T(1,128)S(1)}, s32[1,16]{1,0:T(1,128)}, u32[]{:S(2)}) copy-start(s32[1,16]{1,0:T(1,128)} %param.9) | copy-start | bytes 196
  43.2 43.5 %copy-start.4 = (s32[3,8]{1,0:T(4,128)S(1)}, s32[3,8]{1,0:T(4,128)}, u32[]{:S(2)}) copy-start(s32[3,8]{1,0:T(4,128)} %param.10) | copy-start | bytes 292
  86.7 3.2 %copy-start.5 = (bf16[2,512,648]{2,1,0:T(8,128)(2,1)S(1)}, bf16[2,512,648]{2,1,0:T(8,128)(2,1)}, u32[]{:S(2)}) copy-start(bf16[2,512,648]{2,1,0:T(8,128)(2,1)} %all-gather.3.cloned.1.call-done) | copy-start | bytes 3981316
  89.9 18.9 %copy-start = (f32[2,24,24]{2,1,0:T(8,128)S(1)}, f32[2,24,24]{2,1,0:T(8,128)}, u32[]{:S(2)}) copy-start(f32[2,24,24]{2,1,0:T(8,128)} %param.13) | copy-start | bytes 13828
  90.7 24.9 %copy-start.1 = (f32[1,2,24,24]{3,2,1,0:T(8,128)S(1)}, f32[1,2,24,24]{3,2,1,0:T(8,128)}, u32[]{:S(2)}) copy-start(f32[1,2,24,24]{3,2,1,0:T(8,128)} %param.12) | copy-start | bytes 13828
  92.0 12.1 %all-to-all-start.1 = ((f32[8,1,648]{2,1,0:T(1,128)}), f32[8,1,648]{2,1,0:T(1,128)S(1)}, u32[]{:S(2)}, u32[]{:S(2)}) async-start(f32[8,1,648]{2,1,0:T(1,128)} %reshape.85), calls=%async_computation.1 | async-start | bytes 49152 | tf_op jit(solution)/shard_map/all_to_all | solution.py:82
  104.1 9.9 %all-to-all-start.2 = ((f32[8,1,648]{2,1,0:T(1,128)}), f32[8,1,648]{2,1,0:T(1,128)S(1)}, u32[]{:S(2)}, u32[]{:S(2)}) async-start(f32[8,1,648]{2,1,0:T(1,128)} %reshape.87), calls=%async_computation.2 | async-start | bytes 49152 | tf_op jit(solution)/shard_map/all_to_all | solution.py:83
Sparse Core Ops, SparseCore 0:
  46.0 18.0 all-gather.2
